TPU v7x, 32 devices: a whole 2x2x4 slice. The times are simulated.
32 devices in a mesh: dp: 16 (over z, x, core), tensor: 2 (over y).
Axes of the slice: x: 2, y: 2, z: 4, core: 2. Of those that a mesh axis runs over, the one named last changes fastest.
Arguments:
- tokens: bfloat16 [8192, 1152], P(('dp', 'tensor')), may hold values from -6 to 6
- condition: bfloat16 [32, 1152], P(('dp', 'tensor')), may hold values from -6 to 6
- w_qkv: bfloat16 [1152, 3, 1152], P('dp', None, 'tensor'), may hold values from -0.1875 to 0.1875
- qv_bias: bfloat16 [2, 1152], P(None, 'tensor'), may hold values from -3 to 3
- w_proj: bfloat16 [1152, 1152], P('tensor', 'dp'), may hold values from -1 to 1
- proj_bias: bfloat16 [1152], replicated, may hold values from -3 to 3
- w_fc1: bfloat16 [1152, 4608], P('dp', 'tensor'), may hold values from -0.1875 to 0.1875
- fc1_bias: bfloat16 [4608], P('tensor'), may hold values from -3 to 3
- w_fc2: bfloat16 [4608, 1152], P('tensor', 'dp'), may hold values from -0.09375 to 0.09375
- fc2_bias: bfloat16 [1152], replicated, may hold values from -3 to 3
- w_ada: bfloat16 [1152, 6912], P(None, ('dp', 'tensor')), may hold values from -0.1875 to 0.1875
- ada_bias: bfloat16 [6912], P(('dp', 'tensor')), may hold values from -3 to 3
- cotangent: bfloat16 [8192, 1152], P(('dp', 'tensor')), may hold values from -6 to 6
Outputs:
- output: bfloat16 [8192, 1152], P(('dp', 'tensor'))
- grad_tokens: float32 [8192, 1152], P(('dp', 'tensor'))
- grad_condition: float32 [32, 1152], P(('dp', 'tensor'))
- grad_w_qkv: float32 [1152, 3, 1152], P('dp', None, 'tensor')
- grad_qv_bias: float32 [2, 1152], P(None, 'tensor')
- grad_w_proj: float32 [1152, 1152], P('tensor', 'dp')
- grad_proj_bias: float32 [1152], replicated
- grad_w_fc1: float32 [1152, 4608], P('dp', 'tensor')
- grad_fc1_bias: float32 [4608], P('tensor')
- grad_w_fc2: float32 [4608, 1152], P('tensor', 'dp')
- grad_fc2_bias: float32 [1152], replicated
- grad_w_ada: float32 [1152, 6912], P(None, ('dp', 'tensor'))
- grad_ada_bias: float32 [6912], P(('dp', 'tensor'))
All inputs are finite; a program needn't handle non-finite values.
Results may differ from a plain program's by a relative error of at most 0.015.
The roundings to bfloat16 on the way count: a program that leaves them out, or rounds other values in their place, can miss the bound.
Values may be sent and summed in bfloat16 or wider, within the bound.
A program may use at most 128 MiB of HBM per device.

v0:
```python
from functools import partial
import math

import jax
import jax.numpy as jnp
from jax import lax
from jax.sharding import PartitionSpec as P

HEAD_DIM = 72


eps = 1e-06


def normalize(values):
    center = values - jnp.mean(values, axis=-1, keepdims=True)
    spread = lax.rsqrt(jnp.mean(center * center, axis=-1, keepdims=True) + eps)
    return (center * spread, spread)


def norm_back(gradient, normed, spread):
    return spread * (
        gradient
        - jnp.mean(gradient, axis=-1, keepdims=True)
        - normed * jnp.mean(gradient * normed, axis=-1, keepdims=True)
    )


def contract_last(left_side, right_side):
    return lax.dot_general(
        left_side, right_side, (((1,), (1,)), ((), ())), preferred_element_type=jnp.float32
    )


def contract_first(left_side, right_side):
    return lax.dot_general(
        left_side, right_side, (((0,), (0,)), ((), ())), preferred_element_type=jnp.float32
    )


def gather_rows(values):
    return lax.all_gather(values, "tensor", axis=0, tiled=True)


def gather_grads(values):
    return lax.all_gather(values, "tensor", axis=0, tiled=True)


def sum_rows(source, weight, own_rows):

    def row_term(first_row, number):
        return jnp.dot(source, weight, preferred_element_type=jnp.float32)

    return lax.psum_scatter(
        row_term(jnp.int32(0), lax.axis_size("tensor") * own_rows).astype(jnp.bfloat16),
        "tensor",
        scatter_dimension=0,
        tiled=True,
    ).astype(jnp.float32)


def sum_grads(source, weight, own_rows):

    def row_term(first_row, number):
        return contract_last(source, weight)

    return lax.psum_scatter(
        row_term(jnp.int32(0), lax.axis_size("tensor") * own_rows).astype(jnp.bfloat16),
        "tensor",
        scatter_dimension=0,
        tiled=True,
    ).astype(jnp.float32)


def attend(block):
    query_rows, key_rows, value_rows = block
    scaling = query_rows.shape[-1] ** (-0.5)
    scores = (
        jnp.einsum("sqhe,skhe->shqk", query_rows, key_rows, preferred_element_type=jnp.float32)
        * scaling
    )
    highest = jnp.max(scores, axis=-1, keepdims=True)
    expons = jnp.exp(scores - highest)
    summed = jnp.sum(expons, axis=-1, keepdims=True)
    probs = (expons / summed).astype(jnp.bfloat16)
    mixed = jnp.einsum("shqk,skhe->sqhe", probs, value_rows, preferred_element_type=jnp.float32)
    return (mixed.astype(jnp.bfloat16), (highest + jnp.log(summed))[..., 0])


def attend_back(block):
    query_rows, key_rows, value_rows, logsum, grad_mixed = block
    scaling = query_rows.shape[-1] ** (-0.5)
    scores = (
        jnp.einsum("sqhe,skhe->shqk", query_rows, key_rows, preferred_element_type=jnp.float32)
        * scaling
    )
    probs = jnp.exp(scores - logsum[..., None])
    grad_probs = jnp.einsum(
        "sqhe,skhe->shqk", grad_mixed, value_rows, preferred_element_type=jnp.float32
    )
    grad_values = jnp.einsum(
        "shqk,sqhe->skhe",
        probs.astype(jnp.bfloat16),
        grad_mixed,
        preferred_element_type=jnp.float32,
    )
    grad_scores = (
        probs * (grad_probs - jnp.sum(grad_probs * probs, axis=-1, keepdims=True))
    ).astype(jnp.bfloat16)
    grad_queries = (
        jnp.einsum("shqk,skhe->sqhe", grad_scores, key_rows, preferred_element_type=jnp.float32)
        * scaling
    )
    grad_keys = (
        jnp.einsum("shqk,sqhe->skhe", grad_scores, query_rows, preferred_element_type=jnp.float32)
        * scaling
    )
    return (
        grad_queries.astype(jnp.bfloat16),
        grad_keys.astype(jnp.bfloat16),
        grad_values.astype(jnp.bfloat16),
    )


def per_device(
    tokens,
    condition,
    w_qkv,
    qv_bias,
    w_proj,
    proj_bias,
    w_fc1,
    fc1_bias,
    w_fc2,
    fc2_bias,
    w_ada,
    ada_bias,
    cotangent,
):
    own_rows, width = tokens.shape
    own_seqs = condition.shape[0]
    length = own_rows // own_seqs
    group_rows = own_rows * lax.axis_size("tensor")
    group_seqs = group_rows // length
    local_width = w_qkv.shape[2]
    local_heads = local_width // HEAD_DIM
    block_seqs = math.gcd(group_seqs, max(1, 512 // length))
    blocks = group_seqs // block_seqs
    head_shape = (blocks, block_seqs, length, local_heads, HEAD_DIM)
    cond_float = condition.astype(jnp.float32)
    silu_cond = jax.nn.silu(cond_float).astype(jnp.bfloat16)
    every_cond = lax.all_gather(silu_cond, ("dp", "tensor"), axis=0, tiled=True)
    columns = (
        jnp.dot(every_cond, w_ada, preferred_element_type=jnp.float32)
        + ada_bias.astype(jnp.float32)
    ).astype(jnp.bfloat16)
    modulation = lax.all_to_all(columns, ("dp", "tensor"), split_axis=0, concat_axis=1, tiled=True)
    modul = modulation.astype(jnp.float32).reshape(own_seqs, 6, 1, width)
    shift_attn = modul[:, 0]
    scale_attn = modul[:, 1]
    gate_attn = modul[:, 2]
    shift_mlp = modul[:, 3]
    scale_mlp = modul[:, 4]
    gate_mlp = modul[:, 5]
    qkv_full, proj_full, fc1_full, fc2_full = (
        lax.all_gather(w_qkv, "dp", axis=0, tiled=True),
        lax.all_gather(w_proj, "dp", axis=1, tiled=True),
        lax.all_gather(w_fc1, "dp", axis=0, tiled=True),
        lax.all_gather(w_fc2, "dp", axis=1, tiled=True),
    )
    residual = tokens.astype(jnp.float32).reshape(own_seqs, length, width)
    normed_attn, spread_attn = normalize(residual)
    attn_input = (
        (normed_attn * (1.0 + scale_attn) + shift_attn)
        .astype(jnp.bfloat16)
        .reshape(own_rows, width)
    )
    attn_rows = gather_rows(attn_input)
    projected = jnp.einsum("td,dkf->tkf", attn_rows, qkv_full, preferred_element_type=jnp.float32)
    bias_float = qv_bias.astype(jnp.float32)
    queries = (projected[:, 0] + bias_float[0]).astype(jnp.bfloat16).reshape(head_shape)
    key_all = projected[:, 1].astype(jnp.bfloat16).reshape(head_shape)
    value_all = (projected[:, 2] + bias_float[1]).astype(jnp.bfloat16).reshape(head_shape)
    mixed, logsum = lax.map(attend, (queries, key_all, value_all))
    mixed_rows = mixed.reshape(group_rows, local_width)
    attn_out = (sum_rows(mixed_rows, proj_full, own_rows) + proj_bias.astype(jnp.float32)).reshape(
        own_seqs, length, width
    )
    middle = residual + gate_attn * attn_out
    normed_mlp, spread_mlp = normalize(middle)
    mlp_input = (
        (normed_mlp * (1.0 + scale_mlp) + shift_mlp).astype(jnp.bfloat16).reshape(own_rows, width)
    )
    mlp_rows = gather_rows(mlp_input)
    upper = jnp.dot(mlp_rows, fc1_full, preferred_element_type=jnp.float32) + fc1_bias.astype(
        jnp.float32
    )
    hidden = jax.nn.gelu(upper, approximate=True).astype(jnp.bfloat16)
    mlp_out = (sum_rows(hidden, fc2_full, own_rows) + fc2_bias.astype(jnp.float32)).reshape(
        own_seqs, length, width
    )
    output = (middle + gate_mlp * mlp_out).astype(jnp.bfloat16).reshape(own_rows, width)
    qkv_back, proj_back, fc1_back, fc2_back = (
        lax.all_gather(w_qkv, "dp", axis=0, tiled=True),
        lax.all_gather(w_proj, "dp", axis=1, tiled=True),
        lax.all_gather(w_fc1, "dp", axis=0, tiled=True),
        lax.all_gather(w_fc2, "dp", axis=1, tiled=True),
    )
    grad_out = cotangent.astype(jnp.float32).reshape(own_seqs, length, width)
    grad_mlp = (gate_mlp * grad_out).astype(jnp.bfloat16).reshape(own_rows, width)
    grad_gate_mlp = jnp.sum(grad_out * mlp_out, axis=1)
    grad_mlp_rows = gather_grads(grad_mlp)
    fc2_bias_grad = jnp.sum(grad_mlp_rows.astype(jnp.float32), axis=0)
    fc2_grad = contract_first(hidden, grad_mlp_rows)
    grad_hidden = contract_last(grad_mlp_rows, fc2_back)
    ignored, gelu_pull = jax.vjp(partial(jax.nn.gelu, approximate=True), upper)
    grad_upper = gelu_pull(grad_hidden)[0].astype(jnp.bfloat16)
    fc1_bias_grad = jnp.sum(grad_upper.astype(jnp.float32), axis=0)
    fc1_grad = contract_first(mlp_rows, grad_upper)
    grad_mlp_input = sum_grads(grad_upper, fc1_back, own_rows).reshape(own_seqs, length, width)
    grad_shift_mlp = jnp.sum(grad_mlp_input, axis=1)
    grad_scale_mlp = jnp.sum(grad_mlp_input * normed_mlp, axis=1)
    grad_middle = grad_out + norm_back(grad_mlp_input * (1.0 + scale_mlp), normed_mlp, spread_mlp)
    grad_attn = (gate_attn * grad_middle).astype(jnp.bfloat16).reshape(own_rows, width)
    grad_gate_attn = jnp.sum(grad_middle * attn_out, axis=1)
    grad_attn_rows = gather_grads(grad_attn)
    proj_bias_grad = jnp.sum(grad_attn_rows.astype(jnp.float32), axis=0)
    proj_grad = contract_first(mixed_rows, grad_attn_rows)
    grad_mixed = contract_last(grad_attn_rows, proj_back).astype(jnp.bfloat16).reshape(head_shape)
    grad_query, grad_key, grad_value = lax.map(
        attend_back, (queries, key_all, value_all, logsum, grad_mixed)
    )
    grad_qkv = jnp.stack(
        [
            grad_query.reshape(group_rows, local_width),
            grad_key.reshape(group_rows, local_width),
            grad_value.reshape(group_rows, local_width),
        ],
        axis=1,
    )
    qv_bias_grad = jnp.stack(
        [
            jnp.sum(grad_qkv[:, 0].astype(jnp.float32), axis=0),
            jnp.sum(grad_qkv[:, 2].astype(jnp.float32), axis=0),
        ],
        axis=0,
    )
    qkv_grad = jnp.einsum("td,tkf->dkf", attn_rows, grad_qkv, preferred_element_type=jnp.float32)
    grad_attn_input = sum_grads(
        grad_qkv.reshape(group_rows, 3 * local_width),
        qkv_back.reshape(width, 3 * local_width),
        own_rows,
    ).reshape(own_seqs, length, width)
    grad_shift_attn = jnp.sum(grad_attn_input, axis=1)
    grad_scale_attn = jnp.sum(grad_attn_input * normed_attn, axis=1)
    grad_tokens = (
        grad_middle + norm_back(grad_attn_input * (1.0 + scale_attn), normed_attn, spread_attn)
    ).reshape(own_rows, width)
    grad_modulation = (
        jnp.stack(
            [
                grad_shift_attn,
                grad_scale_attn,
                grad_gate_attn,
                grad_shift_mlp,
                grad_scale_mlp,
                grad_gate_mlp,
            ],
            axis=1,
        )
        .reshape(own_seqs, 6 * width)
        .astype(jnp.bfloat16)
    )
    qkv_grad, proj_grad, fc1_grad, fc2_grad = (
        lax.psum_scatter(qkv_grad, "dp", scatter_dimension=0, tiled=True),
        lax.psum_scatter(proj_grad, "dp", scatter_dimension=1, tiled=True),
        lax.psum_scatter(fc1_grad, "dp", scatter_dimension=0, tiled=True),
        lax.psum_scatter(fc2_grad, "dp", scatter_dimension=1, tiled=True),
    )
    qv_bias_grad, proj_bias_grad, fc1_bias_grad, fc2_bias_grad = lax.psum(
        (qv_bias_grad, proj_bias_grad, fc1_bias_grad, fc2_bias_grad), "dp"
    )
    grad_columns = lax.all_to_all(
        grad_modulation, ("dp", "tensor"), split_axis=1, concat_axis=0, tiled=True
    )
    ada_grad = contract_first(every_cond, grad_columns)
    ada_bias_grad = jnp.sum(grad_columns.astype(jnp.float32), axis=0)
    grad_silu = lax.psum_scatter(
        contract_last(grad_columns, w_ada), ("dp", "tensor"), scatter_dimension=0, tiled=True
    )
    ignored_cond, silu_pull = jax.vjp(jax.nn.silu, cond_float)
    grad_condition = silu_pull(grad_silu)[0]
    return (
        output,
        grad_tokens,
        grad_condition,
        qkv_grad,
        qv_bias_grad,
        proj_grad,
        proj_bias_grad,
        fc1_grad,
        fc1_bias_grad,
        fc2_grad,
        fc2_bias_grad,
        ada_grad,
        ada_bias_grad,
    )


def solution(mesh):
    placed = (
        P(("dp", "tensor"), None),
        P(("dp", "tensor"), None),
        P("dp", None, "tensor"),
        P(None, "tensor"),
        P("tensor", "dp"),
        P(),
        P("dp", "tensor"),
        P("tensor"),
        P("tensor", "dp"),
        P(),
        P(None, ("dp", "tensor")),
        P(("dp", "tensor")),
        P(("dp", "tensor"), None),
    )
    return jax.shard_map(
        per_device,
        mesh=mesh,
        in_specs=placed,
        out_specs=(
            P(("dp", "tensor"), None),
            P(("dp", "tensor"), None),
            P(("dp", "tensor"), None),
            P("dp", None, "tensor"),
            P(None, "tensor"),
            P("tensor", "dp"),
            P(),
            P("dp", "tensor"),
            P("tensor"),
            P("tensor", "dp"),
            P(),
            P(None, ("dp", "tensor")),
            P(("dp", "tensor")),
        ),
        check_vma=False,
    )
```

profile of v0, /device:TPU:0, one launch (start us, length us, event | category | flops | bytes accessed | tf_op | source)
XLA Modules:
  0.0 1101.5 jit_solution(12984828745104131564)
XLA Ops:
  8.0 70.5 %all-gather = bf16[32,1,1152]{2,1,0:T(2,128)(2,1)S(1)} all-gather(bf16[1,1,1152]{2,1,0:T(2,128)(2,1)S(1)} %get-tuple-element.80), channel_id=1, replica_groups=mesh['dp'=16,'tensor'=2] {'dp','tensor'}, dimensions={0}, use_global_device_ids=true | all-gather | bytes 76032 | tf_op jit(solution)/shard_map/all_gather | solution.py:152
  83.2 6.8 all-to-all-done
  93.2 17.5 %all-gather.10.cloned.1.call-done = bf16[512,1152]{1,0:T(8,128)(2,1)} async-done(((bf16[256,1152]{1,0:T(8,128)(2,1)}), bf16[512,1152]{1,0:T(8,128)(2,1)}) %all-gather.10.cloned.1.call-update) | async-done | bytes 1179664 | tf_op jit(solution)/shard_map/all_gather | solution.py:42
  110.7 53.9 %all-gather.12.cloned.1.call-done = bf16[1152,3,576]{2,0,1:T(8,128)(2,1)} async-done(((bf16[72,3,576]{2,0,1:T(8,128)(2,1)}), bf16[1152,3,576]{2,0,1:T(8,128)(2,1)}) %all-gather.12.cloned.1.call-update) | async-done | bytes 3981328 | tf_op jit(solution)/shard_map/all_gather | solution.py:166
  164.6 5.2 fusion.53
  182.3 22.1 %all-gather.14.cloned.1.call-done = bf16[576,1152]{0,1:T(8,128)(2,1)} async-done(((bf16[576,72]{0,1:T(8,128)(2,1)}), bf16[576,1152]{0,1:T(8,128)(2,1)}) %all-gather.14.cloned.1.call-update) | async-done | bytes 1327120 | tf_op jit(solution)/shard_map/all_gather | solution.py:167
  204.4 3.6 convolution_convert_fusion.2
  211.8 17.1 %reduce-scatter.11.cloned.1.call-done = bf16[256,1152]{1,0:T(8,128)(2,1)} async-done(((bf16[512,1152]{1,0:T(8,128)(2,1)}), bf16[256,1152]{1,0:T(8,128)(2,1)}) %reduce-scatter.11.cloned.1.call-update) | async-done | bytes 589840 | tf_op jit(solution)/shard_map/reduce_scatter | solution.py:54
  233.9 19.7 %all-gather.22.cloned.1.call-done = bf16[512,1152]{1,0:T(8,128)(2,1)} async-done(((bf16[256,1152]{1,0:T(8,128)(2,1)}), bf16[512,1152]{1,0:T(8,128)(2,1)}) %all-gather.22.cloned.1.call-update) | async-done | bytes 1179664 | tf_op jit(solution)/shard_map/all_gather | solution.py:46
  253.6 58.4 %all-gather.20.cloned.1.call-done = bf16[2304,1152]{0,1:T(8,128)(2,1)} async-done(((bf16[2304,72]{0,1:T(8,128)(2,1)}), bf16[2304,1152]{0,1:T(8,128)(2,1)}) %all-gather.20.cloned.1.call-update) | async-done | bytes 5308432 | tf_op jit(solution)/shard_map/all_gather | solution.py:169
  312.0 8.2 fusion.89
  320.2 48.9 %all-gather.18.cloned.1.call-done = bf16[1152,2304]{1,0:T(8,128)(2,1)} async-done(((bf16[72,2304]{1,0:T(8,128)(2,1)}), bf16[1152,2304]{1,0:T(8,128)(2,1)}) %all-gather.18.cloned.1.call-update) | async-done | bytes 5308432 | tf_op jit(solution)/shard_map/all_gather | solution.py:168
  369.1 23.5 %all-gather.16.cloned.1.call-done = bf16[512,1152]{1,0:T(8,128)(2,1)} async-done(((bf16[256,1152]{1,0:T(8,128)(2,1)}), bf16[512,1152]{1,0:T(8,128)(2,1)}) %all-gather.16.cloned.1.call-update) | async-done | bytes 1179664 | tf_op jit(solution)/shard_map/all_gather | solution.py:42
  392.6 10.6 convert_reduce_fusion
  404.6 4.2 convolution_convert_fusion
  408.9 9.1 convolution_convert_fusion.1
  418.7 12.1 %reduce-scatter.15.cloned.1.call-done = bf16[256,1152]{1,0:T(8,128)(2,1)} async-done(((bf16[512,1152]{1,0:T(8,128)(2,1)}), bf16[256,1152]{1,0:T(8,128)(2,1)}) %reduce-scatter.15.cloned.1.call-update) | async-done | bytes 589840 | tf_op jit(solution)/shard_map/reduce_scatter | solution.py:67
  433.8 21.0 %reduce-scatter.13.cloned.1.call-done = bf16[256,1152]{1,0:T(8,128)(2,1)} async-done(((bf16[512,1152]{1,0:T(8,128)(2,1)}), bf16[256,1152]{1,0:T(8,128)(2,1)}) %reduce-scatter.13.cloned.1.call-update) | async-done | bytes 589840 | tf_op jit(solution)/shard_map/reduce_scatter | solution.py:54
  454.8 4.0 multiply_reduce_fusion.2
  461.0 22.7 %all-gather.24.cloned.1.call-done = bf16[512,1152]{1,0:T(8,128)(2,1)} async-done(((bf16[256,1152]{1,0:T(8,128)(2,1)}), bf16[512,1152]{1,0:T(8,128)(2,1)}) %all-gather.24.cloned.1.call-update) | async-done | bytes 1179664 | tf_op jit(solution)/shard_map/all_gather | solution.py:46
  503.2 6.2 fusion.8
  510.7 20.8 %reduce-scatter.17.cloned.1.call-done = bf16[256,1152]{1,0:T(8,128)(2,1)} async-done(((bf16[512,1152]{1,0:T(8,128)(2,1)}), bf16[256,1152]{1,0:T(8,128)(2,1)}) %reduce-scatter.17.cloned.1.call-update) | async-done | bytes 589840 | tf_op jit(solution)/shard_map/reduce_scatter | solution.py:67
  534.2 11.8 %all_to_all.26 = bf16[1,32,216]{2,0,1:T(2,128)(2,1)S(1)} all-to-all(bf16[1,32,216]{2,0,1:T(2,128)(2,1)S(1)} %convert_element_type.235), channel_id=1, replica_groups=mesh['dp'=16,'tensor'=2] {'dp','tensor'}, dimensions={1} | all-to-all | bytes 27648 | tf_op jit(solution)/shard_map/all_to_all | solution.py:283
  551.2 7.3 fusion.51
  559.8 8.7 fusion.91
  569.8 9.3 fusion.86
  582.4 58.3 %all-reduce.2 = (f32[2,576]{1,0:T(2,128)}, f32[1152]{0:T(1024)}, f32[2304]{0:T(1024)}, f32[1152]{0:T(1024)}) all-reduce(f32[2,576]{1,0:T(2,128)S(1)} %pad_maximum_fusion, f32[1152]{0:T(1024)S(1)} %convert_reduce_fusion.2, f32[2304]{0:T(1024)S(1)} %copy-done.28, ...), channel_id=1, replica_groups=mesh['dp'=16,'tensor'=2] {'dp'}, use_global_device_ids=true, to_apply=%region_25.26 | all-reduce | flops 5760 | bytes 46080 | tf_op jit(solution)/shard_map/psum | solution.py:280
  644.2 21.4 %all-reduce.5.cloned.1.call-done = f32[32,1152]{1,0:T(8,128)} async-done(((f32[32,1152]{1,0:T(8,128)}), f32[32,1152]{1,0:T(8,128)}) %all-reduce.5.cloned.1.call-update) | async-done | bytes 147472
  667.0 69.2 %reduce-scatter.25.cloned.1.call-done = f32[576,72]{0,1:T(8,128)} async-done(((f32[576,1152]{0,1:T(8,128)}), f32[576,72]{0,1:T(8,128)}) %reduce-scatter.25.cloned.1.call-update) | async-done | bytes 165904
  736.1 109.2 %reduce-scatter.19.cloned.1.call-done = f32[72,3,576]{2,0,1:T(8,128)} async-done(((f32[1152,3,576]{2,0,1:T(8,128)}), f32[72,3,576]{2,0,1:T(8,128)}) %reduce-scatter.19.cloned.1.call-update) | async-done | bytes 497680 | tf_op jit(solution)/shard_map/reduce_scatter | solution.py:275
  845.3 124.5 %reduce-scatter.21.cloned.1.call-done = f32[72,2304]{1,0:T(8,128)} async-done(((f32[1152,2304]{1,0:T(8,128)}), f32[72,2304]{1,0:T(8,128)}) %reduce-scatter.21.cloned.1.call-update) | async-done | bytes 663568 | tf_op jit(solution)/shard_map/reduce_scatter | solution.py:277
  969.8 124.8 %reduce-scatter.23.cloned.1.call-done = f32[2304,72]{0,1:T(8,128)} async-done(((f32[2304,1152]{0,1:T(8,128)}), f32[2304,72]{0,1:T(8,128)}) %reduce-scatter.23.cloned.1.call-update) | async-done | bytes 663568 | tf_op jit(solution)/shard_map/reduce_scatter | solution.py:278
  (186 shorter events, 76.1 us)
Async XLA Ops:
  7.2 71.9 %copy-start = (bf16[1152,216]{0,1:T(8,128)(2,1)S(1)}, bf16[1152,216]{0,1:T(8,128)(2,1)}, u32[]{:S(2)}) copy-start(bf16[1152,216]{0,1:T(8,128)(2,1)} %param.23) | copy-start | bytes 1492996
  7.2 75.5 %copy-start.3 = (bf16[256,1152]{1,0:T(8,128)(2,1)S(1)}, bf16[256,1152]{1,0:T(8,128)(2,1)}, u32[]{:S(2)}) copy-start(bf16[256,1152]{1,0:T(8,128)(2,1)} %param.13) | copy-start | bytes 1769476
  80.1 9.9 all-to-all-start
  82.6 28.0 %all-gather.10.cloned.1.call-start = ((), (), s32[]{:S(2)}) async-start(), calls=%async_computation.10 | async-start | bytes 1769472 | tf_op jit(solution)/shard_map/all_gather | solution.py:42
  83.2 9.7 copy-start.25
  83.2 9.8 copy-start.32
  91.4 73.2 %all-gather.12.cloned.1.call-start = ((), (), s32[]{:S(2)}) async-start(), calls=%async_computation.11 | async-start | bytes 4700160 | tf_op jit(solution)/shard_map/all_gather | solution.py:166
  92.2 112.2 %all-gather.14.cloned.1.call-start = ((), (), s32[]{:S(2)}) async-start(), calls=%async_computation.12 | async-start | bytes 1566720 | tf_op jit(solution)/shard_map/all_gather | solution.py:167
  92.9 136.0 %reduce-scatter.11.cloned.1.call-start = ((), (), s32[]{:S(2)}) async-start(), calls=%async_computation.13 | async-start | bytes 1769472 | tf_op jit(solution)/shard_map/reduce_scatter | solution.py:54
  182.3 25.7 %copy-start.12 = (bf16[72,8,2,256]{3,1,2,0:T(8,128)(2,1)}, bf16[72,8,2,256]{3,1,2,0:T(8,128)(2,1)S(1)}, u32[]{:S(2)}) copy-start(bf16[72,8,2,256]{3,1,2,0:T(8,128)(2,1)S(1)} %copy.93) | copy-start | bytes 1769476
  208.1 45.6 %all-gather.22.cloned.1.call-start = ((), (), s32[]{:S(2)}) async-start(), calls=%async_computation.18 | async-start | bytes 1769472 | tf_op jit(solution)/shard_map/all_gather | solution.py:46
  210.0 101.9 %all-gather.20.cloned.1.call-start = ((), (), s32[]{:S(2)}) async-start(), calls=%async_computation.16 | async-start | bytes 5640192 | tf_op jit(solution)/shard_map/all_gather | solution.py:169
  210.6 158.5 %all-gather.18.cloned.1.call-start = ((), (), s32[]{:S(2)}) async-start(), calls=%async_computation.15 | async-start | bytes 5640192 | tf_op jit(solution)/shard_map/all_gather | solution.py:168
  211.4 181.2 %all-gather.16.cloned.1.call-start = ((), (), s32[]{:S(2)}) async-start(), calls=%async_computation.14 | async-start | bytes 1769472 | tf_op jit(solution)/shard_map/all_gather | solution.py:42
  232.6 198.3 %reduce-scatter.15.cloned.1.call-start = ((), (), s32[]{:S(2)}) async-start(), calls=%async_computation.19 | async-start | bytes 1769472 | tf_op jit(solution)/shard_map/reduce_scatter | solution.py:67
  392.6 12.0 %copy-start.33 = (bf16[1152,2304]{1,0:T(8,128)(2,1)S(1)}, bf16[1152,2304]{1,0:T(8,128)(2,1)}, u32[]{:S(2)}) copy-start(bf16[1152,2304]{1,0:T(8,128)(2,1)} %all-gather.18.cloned.1.call-done) | copy-start | bytes 15925252
  408.8 46.0 %reduce-scatter.13.cloned.1.call-start = ((), (), s32[]{:S(2)}) async-start(), calls=%async_computation.17 | async-start | bytes 1769472 | tf_op jit(solution)/shard_map/reduce_scatter | solution.py:54
  418.0 65.7 %all-gather.24.cloned.1.call-start = ((), (), s32[]{:S(2)}) async-start(), calls=%async_computation.20 | async-start | bytes 1769472 | tf_op jit(solution)/shard_map/all_gather | solution.py:46
  460.7 70.7 %reduce-scatter.17.cloned.1.call-start = ((), (), s32[]{:S(2)}) async-start(), calls=%async_computation.21 | async-start | bytes 1769472 | tf_op jit(solution)/shard_map/reduce_scatter | solution.py:67
  509.4 22.0 %copy-start.26 = (f32[256]{0:T(256)S(1)}, f32[256]{0:T(256)}, u32[]{:S(2)}) copy-start(f32[256]{0:T(256)} %copy-done.25) | copy-start | bytes 3076
  509.5 156.1 %all-reduce.5.cloned.1.call-start = ((), (), s32[]{:S(2)}) async-start(), calls=%async_computation.25 | async-start | bytes 294912
  510.7 36.2 %copy-start.13 = (bf16[72,8,2,256]{3,1,2,0:T(8,128)(2,1)S(1)}, bf16[72,8,2,256]{3,1,2,0:T(8,128)(2,1)}, u32[]{:S(2)}) copy-start(bf16[72,8,2,256]{3,1,2,0:T(8,128)(2,1)} %copy-done.12) | copy-start | bytes 1769476
  531.5 15.4 %copy-start.9 = (bf16[512,1152]{1,0:T(8,128)(2,1)S(1)}, bf16[512,1152]{1,0:T(8,128)(2,1)}, u32[]{:S(2)}) copy-start(bf16[512,1152]{1,0:T(8,128)(2,1)} %all-gather.24.cloned.1.call-done) | copy-start | bytes 3538948
  546.8 189.3 %reduce-scatter.25.cloned.1.call-start = ((), (), s32[]{:S(2)}) async-start(), calls=%async_computation.26 | async-start | bytes 3133440
  549.8 295.5 %reduce-scatter.19.cloned.1.call-start = ((), (), s32[]{:S(2)}) async-start(), calls=%async_computation.22 | async-start | bytes 9400320 | tf_op jit(solution)/shard_map/reduce_scatter | solution.py:275
  558.6 411.2 %reduce-scatter.21.cloned.1.call-start = ((), (), s32[]{:S(2)}) async-start(), calls=%async_computation.23 | async-start | bytes 11280384 | tf_op jit(solution)/shard_map/reduce_scatter | solution.py:277
  568.5 526.1 %reduce-scatter.23.cloned.1.call-start = ((), (), s32[]{:S(2)}) async-start(), calls=%async_computation.24 | async-start | bytes 11280384 | tf_op jit(solution)/shard_map/reduce_scatter | solution.py:278
  579.1 61.6 %copy-start.30 = (f32[256]{0:T(256)S(1)}, f32[256]{0:T(256)}, u32[]{:S(2)}) copy-start(f32[256]{0:T(256)} %get-tuple-element.61) | copy-start | bytes 3076
  579.1 61.6 %copy-start.29 = (f32[256]{0:T(256)S(1)}, f32[256]{0:T(256)}, u32[]{:S(2)}) copy-start(f32[256]{0:T(256)} %get-tuple-element.62) | copy-start | bytes 3076
  579.2 61.6 %copy-start.6 = (f32[256,1152]{1,0:T(8,128)S(1)}, f32[256,1152]{1,0:T(8,128)}, u32[]{:S(2)}) copy-start(f32[256,1152]{1,0:T(8,128)} %copy-done.5) | copy-start | bytes 3538948
  579.2 61.6 %copy-start.27 = (f32[256]{0:T(256)S(1)}, f32[256]{0:T(256)}, u32[]{:S(2)}) copy-start(f32[256]{0:T(256)} %copy-done.25) | copy-start | bytes 3076
  640.8 24.8 %copy-start.20 = (bf16[1,1152]{1,0:T(2,128)(2,1)S(1)}, bf16[1,1152]{1,0:T(2,128)(2,1)}, u32[]{:S(2)}) copy-start(bf16[1,1152]{1,0:T(2,128)(2,1)} %param.14) | copy-start | bytes 6916
  (22 other events, 36.4 us)
Sparse Core Ops, SparseCore 0:
  91.5 19.0 all-gather.9
  112.9 51.6 all-gather.11
  166.7 37.6 all-gather.13
  208.2 20.6 reduce-scatter.10
  230.8 22.7 all-gather.21
  255.6 56.2 all-gather.19
  314.1 54.9 all-gather.17
  371.2 21.3 all-gather.15
  409.0 21.8 reduce-scatter.14
  432.9 21.8 reduce-scatter.12
  460.9 22.7 all-gather.23
  509.6 21.8 reduce-scatter.16
  546.9 118.5 all-reduce.4
  669.9 66.1 reduce-scatter.24
  740.7 104.5 reduce-scatter.18
  849.8 119.9 reduce-scatter.20
  974.3 120.2 reduce-scatter.22
where the time goes:
time: 1110 us; the launch traced here: 1100 us
  waiting for transfers between devices  796 us (72%)
  blocking collectives  141 us (13%)
  matrix products  90.2 us (8%)
  other arithmetic  28 us (3%)
  local copies, waits for them, and re-layouts  27.5 us (2%)
  between operations  14.9 us (1%)
    reduce_scatter x1, waiting for transfers between devices, per_device(): lax.psum_scatter(fc2_grad, 'dp', scatter_dimension=1, tiled=True)  125 us
    reduce_scatter x1, waiting for transfers between devices, per_device(): lax.psum_scatter(fc1_grad, 'dp', scatter_dimension=0, tiled=True)  124 us
    reduce_scatter x1, waiting for transfers between devices, per_device(): lax.psum_scatter(qkv_grad, 'dp', scatter_dimension=0, tiled=True)  109 us
    unnamed x19, waiting for transfers between devices  93.4 us
    all_gather x1, blocking collectives, per_device(): every_cond = lax.all_gather(silu_cond, ('dp', 'tensor'), axis=0, tiled=True)  70.5 us
    all_gather x1, waiting for transfers between devices, per_device(): lax.all_gather(w_fc2, 'dp', axis=1, tiled=True)  58.4 us
    psum x1, blocking collectives, per_device(): lax.psum((qv_bias_grad, proj_bias_grad, fc1_bias_grad, fc2_bias_grad), 'dp')  58.3 us
    all_gather x1, waiting for transfers between devices, per_device(): lax.all_gather(w_qkv, 'dp', axis=0, tiled=True)  53.9 us
  transfers between devices with their start and end apart: 18, of which 18 were waited for; matrix products, arithmetic and copies ran while one was open for 7% of the time, Pallas kernels for 0%

commit v1 on v0

--- a/solution.py
+++ b/solution.py
@@ -272,10 +272,10 @@
         .astype(jnp.bfloat16)
     )
     qkv_grad, proj_grad, fc1_grad, fc2_grad = (
-        lax.psum_scatter(qkv_grad, "dp", scatter_dimension=0, tiled=True),
-        lax.psum_scatter(proj_grad, "dp", scatter_dimension=1, tiled=True),
-        lax.psum_scatter(fc1_grad, "dp", scatter_dimension=0, tiled=True),
-        lax.psum_scatter(fc2_grad, "dp", scatter_dimension=1, tiled=True),
+        lax.psum_scatter(qkv_grad.astype(jnp.bfloat16), "dp", scatter_dimension=0, tiled=True).astype(jnp.float32),
+        lax.psum_scatter(proj_grad.astype(jnp.bfloat16), "dp", scatter_dimension=1, tiled=True).astype(jnp.float32),
+        lax.psum_scatter(fc1_grad.astype(jnp.bfloat16), "dp", scatter_dimension=0, tiled=True).astype(jnp.float32),
+        lax.psum_scatter(fc2_grad.astype(jnp.bfloat16), "dp", scatter_dimension=1, tiled=True).astype(jnp.float32),
     )
     qv_bias_grad, proj_bias_grad, fc1_bias_grad, fc2_bias_grad = lax.psum(
         (qv_bias_grad, proj_bias_grad, fc1_bias_grad, fc2_bias_grad), "dp"

time: 1110 us -> 978 us (0.88)
  waiting for transfers between devices: 796 us -> 632 us
  local copies, waits for them, and re-layouts: 27.5 us -> 58.4 us
    reduce_scatter x3 -> x2, waiting for transfers between devices: 358 us -> 162 us  [the longest x1 82.7 us: per_device(): lax.psum_scatter(fc1_grad.astype(jnp.bfloat16), 'dp', scatter_dimension=0...]
    unnamed x19 -> x20, waiting for transfers between devices: 93.4 us -> 130 us
    unnamed x75 -> x74, local copies, waits for them, and re-layouts: 11.8 us -> 42.7 us
  transfers between devices with their start and end apart: 18 -> 18, of which waited for: 18 -> 17; matrix products, arithmetic and copies ran while one was open for 7% -> 11% of each run, Pallas kernels for 0% -> 0%
where the time goes in v1:
time: 978 us; the launch traced here: 968 us
  waiting for transfers between devices  632 us (65%)
  blocking collectives  141 us (14%)
  matrix products  84 us (9%)
  local copies, waits for them, and re-layouts  58.4 us (6%)
  other arithmetic  33.6 us (3%)
  between operations  14.9 us (2%)
    unnamed x20, waiting for transfers between devices  130 us
    reduce_scatter x1, waiting for transfers between devices, per_device(): lax.psum_scatter(fc1_grad.astype(jnp.bfloat16), 'dp', scatter_dimension=0...  82.7 us
    reduce_scatter x1, waiting for transfers between devices, per_device(): lax.psum_scatter(fc2_grad.astype(jnp.bfloat16), 'dp', scatter_dimension=1...  79.1 us
    all_gather x1, blocking collectives, per_device(): every_cond = lax.all_gather(silu_cond, ('dp', 'tensor'), axis=0, tiled=True)  70.5 us
    psum x1, blocking collectives, per_device(): lax.psum((qv_bias_grad, proj_bias_grad, fc1_bias_grad, fc2_bias_grad), 'dp')  58.4 us
    all_gather x1, waiting for transfers between devices, per_device(): lax.all_gather(w_fc2, 'dp', axis=1, tiled=True)  58.4 us
    all_gather x1, waiting for transfers between devices, per_device(): lax.all_gather(w_qkv, 'dp', axis=0, tiled=True)  53.9 us
    all_gather x1, waiting for transfers between devices, per_device(): lax.all_gather(w_fc1, 'dp', axis=0, tiled=True)  48.9 us
  transfers between devices with their start and end apart: 18, of which 17 were waited for; matrix products, arithmetic and copies ran while one was open for 11% of the time, Pallas kernels for 0%

profile of v1, /device:TPU:0, one launch (start us, length us, event | category | flops | bytes accessed | tf_op | source)
XLA Modules:
  0.0 968.3 jit_solution(9200574821584645337)
XLA Ops:
  8.0 70.5 %all-gather = bf16[32,1,1152]{2,1,0:T(2,128)(2,1)S(1)} all-gather(bf16[1,1,1152]{2,1,0:T(2,128)(2,1)S(1)} %get-tuple-element.80), channel_id=1, replica_groups=mesh['dp'=16,'tensor'=2] {'dp','tensor'}, dimensions={0}, use_global_device_ids=true | all-gather | bytes 76032 | tf_op jit(solution)/shard_map/all_gather | solution.py:152
  83.2 6.8 all-to-all-done
  93.2 17.5 %all-gather.10.cloned.1.call-done = bf16[512,1152]{1,0:T(8,128)(2,1)} async-done(((bf16[256,1152]{1,0:T(8,128)(2,1)}), bf16[512,1152]{1,0:T(8,128)(2,1)}) %all-gather.10.cloned.1.call-update) | async-done | bytes 1179664 | tf_op jit(solution)/shard_map/all_gather | solution.py:42
  110.7 53.9 %all-gather.12.cloned.1.call-done = bf16[1152,3,576]{2,0,1:T(8,128)(2,1)} async-done(((bf16[72,3,576]{2,0,1:T(8,128)(2,1)}), bf16[1152,3,576]{2,0,1:T(8,128)(2,1)}) %all-gather.12.cloned.1.call-update) | async-done | bytes 3981328 | tf_op jit(solution)/shard_map/all_gather | solution.py:166
  164.6 5.2 fusion.52
  182.3 22.1 %all-gather.14.cloned.1.call-done = bf16[576,1152]{0,1:T(8,128)(2,1)} async-done(((bf16[576,72]{0,1:T(8,128)(2,1)}), bf16[576,1152]{0,1:T(8,128)(2,1)}) %all-gather.14.cloned.1.call-update) | async-done | bytes 1327120 | tf_op jit(solution)/shard_map/all_gather | solution.py:167
  211.8 17.1 %reduce-scatter.13.cloned.1.call-done = bf16[256,1152]{1,0:T(8,128)(2,1)} async-done(((bf16[512,1152]{1,0:T(8,128)(2,1)}), bf16[256,1152]{1,0:T(8,128)(2,1)}) %reduce-scatter.13.cloned.1.call-update) | async-done | bytes 589840 | tf_op jit(solution)/shard_map/reduce_scatter | solution.py:54
  233.9 19.7 %all-gather.22.cloned.1.call-done = bf16[512,1152]{1,0:T(8,128)(2,1)} async-done(((bf16[256,1152]{1,0:T(8,128)(2,1)}), bf16[512,1152]{1,0:T(8,128)(2,1)}) %all-gather.22.cloned.1.call-update) | async-done | bytes 1179664 | tf_op jit(solution)/shard_map/all_gather | solution.py:46
  253.6 58.4 %all-gather.20.cloned.1.call-done = bf16[2304,1152]{0,1:T(8,128)(2,1)} async-done(((bf16[2304,72]{0,1:T(8,128)(2,1)}), bf16[2304,1152]{0,1:T(8,128)(2,1)}) %all-gather.20.cloned.1.call-update) | async-done | bytes 5308432 | tf_op jit(solution)/shard_map/all_gather | solution.py:169
  312.0 8.2 fusion.87
  320.2 48.9 %all-gather.18.cloned.1.call-done = bf16[1152,2304]{1,0:T(8,128)(2,1)} async-done(((bf16[72,2304]{1,0:T(8,128)(2,1)}), bf16[1152,2304]{1,0:T(8,128)(2,1)}) %all-gather.18.cloned.1.call-update) | async-done | bytes 5308432 | tf_op jit(solution)/shard_map/all_gather | solution.py:168
  369.1 23.5 %all-gather.16.cloned.1.call-done = bf16[512,1152]{1,0:T(8,128)(2,1)} async-done(((bf16[256,1152]{1,0:T(8,128)(2,1)}), bf16[512,1152]{1,0:T(8,128)(2,1)}) %all-gather.16.cloned.1.call-update) | async-done | bytes 1179664 | tf_op jit(solution)/shard_map/all_gather | solution.py:42
  392.6 10.6 %convert_reduce_fusion = (f32[2304]{0:T(1024)}, bf16[512,2304]{1,0:T(8,128)(2,1)S(1)}, f32[512,2304]{1,0:T(8,128)}) fusion(f32[512,2304]{1,0:T(8,128)} %fusion.87, f32[2304]{0:T(1024)} %convert_element_type.228, bf16[512,1152]{1,0:T(8,128)(2,1)} %all-gather.16.cloned.1.call-done, bf16[1152,2304]{1,0:T(8,128)(2,1)} %all-gather.18.cloned.1.call-done), kind=kOutput, calls=%fused_computation.13 | convolution fusion | flops 2745038592 | bytes 18302976 | tf_op jit(solution)/shard_map/dot_general | solution.py:195
  404.7 4.2 convolution_convert_fusion.4
  409.0 9.0 convolution_convert_fusion.5
  418.8 12.1 %reduce-scatter.17.cloned.1.call-done = bf16[256,1152]{1,0:T(8,128)(2,1)} async-done(((bf16[512,1152]{1,0:T(8,128)(2,1)}), bf16[256,1152]{1,0:T(8,128)(2,1)}) %reduce-scatter.17.cloned.1.call-update) | async-done | bytes 589840 | tf_op jit(solution)/shard_map/reduce_scatter | solution.py:67
  433.9 21.0 %reduce-scatter.15.cloned.1.call-done = bf16[256,1152]{1,0:T(8,128)(2,1)} async-done(((bf16[512,1152]{1,0:T(8,128)(2,1)}), bf16[256,1152]{1,0:T(8,128)(2,1)}) %reduce-scatter.15.cloned.1.call-update) | async-done | bytes 589840 | tf_op jit(solution)/shard_map/reduce_scatter | solution.py:54
  454.9 4.0 multiply_reduce_fusion.2
  461.1 22.7 %all-gather.24.cloned.1.call-done = bf16[512,1152]{1,0:T(8,128)(2,1)} async-done(((bf16[256,1152]{1,0:T(8,128)(2,1)}), bf16[512,1152]{1,0:T(8,128)(2,1)}) %all-gather.24.cloned.1.call-update) | async-done | bytes 1179664 | tf_op jit(solution)/shard_map/all_gather | solution.py:46
  503.5 6.3 fusion.8
  514.6 17.2 %reduce-scatter.19.cloned.1.call-done = bf16[256,1152]{1,0:T(8,128)(2,1)} async-done(((bf16[512,1152]{1,0:T(8,128)(2,1)}), bf16[256,1152]{1,0:T(8,128)(2,1)}) %reduce-scatter.19.cloned.1.call-update) | async-done | bytes 589840 | tf_op jit(solution)/shard_map/reduce_scatter | solution.py:67
  534.0 11.8 %all_to_all.26 = bf16[1,32,216]{2,0,1:T(2,128)(2,1)S(1)} all-to-all(bf16[1,32,216]{2,0,1:T(2,128)(2,1)S(1)} %convert_element_type.267), channel_id=1, replica_groups=mesh['dp'=16,'tensor'=2] {'dp','tensor'}, dimensions={1} | all-to-all | bytes 27648 | tf_op jit(solution)/shard_map/all_to_all | solution.py:283
  546.7 7.1 convolution_convert_fusion.1
  555.1 7.7 convolution_convert_fusion
  564.1 4.1 convolution_convert_fusion.2
  568.2 18.2 %copy.91 = bf16[1152,3,576]{2,1,0:T(4,128)(2,1)} copy(bf16[1152,3,576]{2,0,1:T(8,128)(2,1)S(1)} %convolution_convert_fusion.2) | data formatting | bytes 7962624
  586.5 12.3 %reshape.316 = bf16[1152,1728]{1,0:T(8,128)(2,1)} reshape(bf16[1152,3,576]{2,1,0:T(4,128)(2,1)} %copy.91) | data formatting | bytes 7962624
  602.1 58.4 %all-reduce.2 = (f32[2,576]{1,0:T(2,128)}, f32[1152]{0:T(1024)}, f32[2304]{0:T(1024)}, f32[1152]{0:T(1024)}) all-reduce(f32[2,576]{1,0:T(2,128)S(1)} %pad_maximum_fusion, f32[1152]{0:T(1024)S(1)} %convert_reduce_fusion.2, f32[2304]{0:T(1024)S(1)} %copy-done.27, ...), channel_id=1, replica_groups=mesh['dp'=16,'tensor'=2] {'dp'}, use_global_device_ids=true, to_apply=%region_25.26 | all-reduce | flops 5760 | bytes 46080 | tf_op jit(solution)/shard_map/psum | solution.py:280
  665.4 55.3 %all-reduce.5.cloned.1.call-done = f32[32,1152]{1,0:T(8,128)} async-done(((f32[32,1152]{1,0:T(8,128)}), f32[32,1152]{1,0:T(8,128)}) %all-reduce.5.cloned.1.call-update) | async-done | bytes 147472
  722.1 82.7 %reduce-scatter.21.cloned.1.call-done = bf16[72,2304]{1,0:T(8,128)(2,1)} async-done(((bf16[1152,2304]{1,0:T(8,128)(2,1)}), bf16[72,2304]{1,0:T(8,128)(2,1)}) %reduce-scatter.21.cloned.1.call-update) | async-done | bytes 331792 | tf_op jit(solution)/shard_map/reduce_scatter | solution.py:277
  806.6 79.1 %reduce-scatter.23.cloned.1.call-done = bf16[2304,72]{0,1:T(8,128)(2,1)} async-done(((bf16[2304,1152]{0,1:T(8,128)(2,1)}), bf16[2304,72]{0,1:T(8,128)(2,1)}) %reduce-scatter.23.cloned.1.call-update) | async-done | bytes 331792 | tf_op jit(solution)/shard_map/reduce_scatter | solution.py:278
  887.6 71.7 %reduce-scatter.25.cloned.1.call-done = bf16[72,1728]{1,0:T(8,128)(2,1)} async-done(((bf16[1152,1728]{1,0:T(8,128)(2,1)}), bf16[72,1728]{1,0:T(8,128)(2,1)}) %reduce-scatter.25.cloned.1.call-update) | async-done | bytes 248848
  (189 shorter events, 86.0 us)
Async XLA Ops:
  7.2 71.9 %copy-start = (bf16[1152,216]{0,1:T(8,128)(2,1)S(1)}, bf16[1152,216]{0,1:T(8,128)(2,1)}, u32[]{:S(2)}) copy-start(bf16[1152,216]{0,1:T(8,128)(2,1)} %param.23) | copy-start | bytes 1492996
  7.2 75.5 %copy-start.3 = (bf16[256,1152]{1,0:T(8,128)(2,1)S(1)}, bf16[256,1152]{1,0:T(8,128)(2,1)}, u32[]{:S(2)}) copy-start(bf16[256,1152]{1,0:T(8,128)(2,1)} %param.13) | copy-start | bytes 1769476
  80.1 9.9 %all-to-all-start = ((bf16[32,1,216]{2,1,0:T(2,128)(2,1)}), bf16[32,1,216]{2,1,0:T(2,128)(2,1)S(1)}, u32[]{:S(2)}, u32[]{:S(2)}) async-start(bf16[32,1,216]{2,1,0:T(2,128)(2,1)} %copy.68), calls=%async_computation | async-start | bytes 65536 | tf_op jit(solution)/shard_map/all_to_all | solution.py:157
  82.6 28.0 %all-gather.10.cloned.1.call-start = ((), (), s32[]{:S(2)}) async-start(), calls=%async_computation.10 | async-start | bytes 1769472 | tf_op jit(solution)/shard_map/all_gather | solution.py:42
  83.2 9.7 %copy-start.25 = (f32[256]{0:T(256)}, f32[256]{0:T(256)S(1)}, u32[]{:S(2)}) copy-start(f32[256]{0:T(256)S(1)} %add_rsqrt_fusion.1) | copy-start | bytes 3076
  83.2 9.8 %copy-start.29 = (bf16[2,576]{1,0:T(2,128)(2,1)S(1)}, bf16[2,576]{1,0:T(2,128)(2,1)}, u32[]{:S(2)}) copy-start(bf16[2,576]{1,0:T(2,128)(2,1)} %param.16) | copy-start | bytes 6916
  91.4 73.2 %all-gather.12.cloned.1.call-start = ((), (), s32[]{:S(2)}) async-start(), calls=%async_computation.11 | async-start | bytes 4700160 | tf_op jit(solution)/shard_map/all_gather | solution.py:166
  92.2 112.2 %all-gather.14.cloned.1.call-start = ((), (), s32[]{:S(2)}) async-start(), calls=%async_computation.12 | async-start | bytes 1566720 | tf_op jit(solution)/shard_map/all_gather | solution.py:167
  92.9 135.9 %reduce-scatter.13.cloned.1.call-start = ((), (), s32[]{:S(2)}) async-start(), calls=%async_computation.13 | async-start | bytes 1769472 | tf_op jit(solution)/shard_map/reduce_scatter | solution.py:54
  182.3 22.1 %copy-start.16 = (bf16[72,8,2,256]{3,1,2,0:T(8,128)(2,1)}, bf16[72,8,2,256]{3,1,2,0:T(8,128)(2,1)S(1)}, u32[]{:S(2)}) copy-start(bf16[72,8,2,256]{3,1,2,0:T(8,128)(2,1)S(1)} %copy.95) | copy-start | bytes 1769476
  208.0 45.6 %all-gather.22.cloned.1.call-start = ((), (), s32[]{:S(2)}) async-start(), calls=%async_computation.18 | async-start | bytes 1769472 | tf_op jit(solution)/shard_map/all_gather | solution.py:46
  210.0 101.9 %all-gather.20.cloned.1.call-start = ((), (), s32[]{:S(2)}) async-start(), calls=%async_computation.16 | async-start | bytes 5640192 | tf_op jit(solution)/shard_map/all_gather | solution.py:169
  210.6 158.5 %all-gather.18.cloned.1.call-start = ((), (), s32[]{:S(2)}) async-start(), calls=%async_computation.15 | async-start | bytes 5640192 | tf_op jit(solution)/shard_map/all_gather | solution.py:168
  211.4 181.2 %all-gather.16.cloned.1.call-start = ((), (), s32[]{:S(2)}) async-start(), calls=%async_computation.14 | async-start | bytes 1769472 | tf_op jit(solution)/shard_map/all_gather | solution.py:42
  232.6 198.4 %reduce-scatter.17.cloned.1.call-start = ((), (), s32[]{:S(2)}) async-start(), calls=%async_computation.19 | async-start | bytes 1769472 | tf_op jit(solution)/shard_map/reduce_scatter | solution.py:67
  392.6 12.1 %copy-start.30 = (bf16[1152,2304]{1,0:T(8,128)(2,1)S(1)}, bf16[1152,2304]{1,0:T(8,128)(2,1)}, u32[]{:S(2)}) copy-start(bf16[1152,2304]{1,0:T(8,128)(2,1)} %all-gather.18.cloned.1.call-done) | copy-start | bytes 15925252
  408.9 46.0 %reduce-scatter.15.cloned.1.call-start = ((), (), s32[]{:S(2)}) async-start(), calls=%async_computation.17 | async-start | bytes 1769472 | tf_op jit(solution)/shard_map/reduce_scatter | solution.py:54
  418.0 65.7 %all-gather.24.cloned.1.call-start = ((), (), s32[]{:S(2)}) async-start(), calls=%async_computation.20 | async-start | bytes 1769472 | tf_op jit(solution)/shard_map/all_gather | solution.py:46
  460.8 71.0 %reduce-scatter.19.cloned.1.call-start = ((), (), s32[]{:S(2)}) async-start(), calls=%async_computation.21 | async-start | bytes 1769472 | tf_op jit(solution)/shard_map/reduce_scatter | solution.py:67
  489.2 4.0 copy-start.2
  489.2 4.0 copy-start.10
  503.5 6.6 copy-start.17
  509.9 150.6 %reduce-scatter.27.cloned.1.call-start = ((), (), s32[]{:S(2)}) async-start(), calls=%async_computation.26 | async-start | bytes 1566720
  513.4 18.4 %copy-start.26 = (f32[256]{0:T(256)S(1)}, f32[256]{0:T(256)}, u32[]{:S(2)}) copy-start(f32[256]{0:T(256)} %copy-done.25) | copy-start | bytes 3076
  513.5 207.3 %all-reduce.5.cloned.1.call-start = ((), (), s32[]{:S(2)}) async-start(), calls=%async_computation.25 | async-start | bytes 294912
  531.8 14.9 %copy-start.32 = (bf16[512,1152]{1,0:T(8,128)(2,1)S(1)}, bf16[512,1152]{1,0:T(8,128)(2,1)}, u32[]{:S(2)}) copy-start(bf16[512,1152]{1,0:T(8,128)(2,1)} %all-gather.16.cloned.1.call-done) | copy-start | bytes 3538948
  546.7 258.1 %reduce-scatter.21.cloned.1.call-start = ((), (), s32[]{:S(2)}) async-start(), calls=%async_computation.22 | async-start | bytes 5640192 | tf_op jit(solution)/shard_map/reduce_scatter | solution.py:277
  553.9 331.9 %reduce-scatter.23.cloned.1.call-start = ((), (), s32[]{:S(2)}) async-start(), calls=%async_computation.23 | async-start | bytes 5640192 | tf_op jit(solution)/shard_map/reduce_scatter | solution.py:278
  562.9 396.4 %reduce-scatter.25.cloned.1.call-start = ((), (), s32[]{:S(2)}) async-start(), calls=%async_computation.24 | async-start | bytes 4386816
  598.8 3.3 copy-start.27
  598.8 63.2 %copy-start.6 = (f32[256,1152]{1,0:T(8,128)S(1)}, f32[256,1152]{1,0:T(8,128)}, u32[]{:S(2)}) copy-start(f32[256,1152]{1,0:T(8,128)} %copy-done.5) | copy-start | bytes 3538948
  662.1 58.7 %copy-start.19 = (bf16[1,1152]{1,0:T(2,128)(2,1)S(1)}, bf16[1,1152]{1,0:T(2,128)(2,1)}, u32[]{:S(2)}) copy-start(bf16[1,1152]{1,0:T(2,128)(2,1)} %param.14) | copy-start | bytes 6916
  (20 other events, 26.8 us)
Sparse Core Ops, SparseCore 0:
  91.5 19.0 all-gather.9
  112.9 51.6 all-gather.11
  166.7 37.6 all-gather.13
  208.2 20.6 reduce-scatter.12
  230.8 22.7 all-gather.21
  255.6 56.2 all-gather.19
  314.1 54.9 all-gather.17
  371.2 21.3 all-gather.15
  409.1 21.8 reduce-scatter.16
  433.0 21.8 reduce-scatter.14
  461.0 22.7 all-gather.23
  510.0 21.8 reduce-scatter.18
  535.6 57.8 reduce-scatter.26
  599.5 121.2 all-reduce.4
  724.6 80.1 reduce-scatter.20
  808.7 77.0 reduce-scatter.22
  889.5 69.7 reduce-scatter.24
